TPU v7x, 32 devices: a whole 2x2x4 slice. The times are simulated.
32 devices in a mesh: seq: 8 (over z, x), head: 4 (over y, core).
Axes of the slice: x: 2, y: 2, z: 4, core: 2. Of those that a mesh axis runs over, the one named last changes fastest.
Arguments:
- query_in: bfloat16 [2048, 8192], P('seq', 'head'), may hold values from -1.796875 to 1.796875
- key_in: bfloat16 [2048, 8192], P('seq', 'head'), may hold values from -1.796875 to 1.796875
- value_in: bfloat16 [2048, 8192], P('seq', 'head'), may hold values from -11 to 11
- log_decay: float32 [2048, 64], P('seq', 'head'), may hold values from -1 to 0, as said below
- norm_gain: float32 [8192], P('head'), may hold values from 0.5 to 1.5
- prompt_lengths: int32 [4], replicated, may hold values from 1 to 1536, 2048 in all
- step_query: bfloat16 [4, 128, 8192], P(None, 'seq', 'head'), may hold values from -1.796875 to 1.796875
- step_key: bfloat16 [4, 128, 8192], P(None, 'seq', 'head'), may hold values from -1.796875 to 1.796875
- step_value: bfloat16 [4, 128, 8192], P(None, 'seq', 'head'), may hold values from -6 to 6
- step_decay: float32 [4, 128, 64], P(None, 'seq', 'head'), may hold values from -0.3 to -0.01
- row_prompt: int32 [128], P('seq'), may hold values from 0 to 3
Outputs:
- attn_out: bfloat16 [2048, 8192], P('seq', 'head')
- decode_out: bfloat16 [4, 128, 8192], P(None, 'seq', 'head')
Inputs may be any that keep to these rules, and one draw needn't show every extreme that they name: `log_decay`: Negative; per head and token.
All inputs are finite; a program needn't handle non-finite values.
Results may differ from a plain program's by a relative error of at most 0.0056.
Values sent between devices are 32-bit elements; how exact they have to be, the bound alone decides.
A program may use at most 64 MiB of HBM per device.

v0:
```python
import jax
import jax.numpy as jnp
from jax import lax
from jax.sharding import PartitionSpec as P

HEAD_COUNT = 64
HDIM = 128
BLOCK = 256
PROMPTS = 4
EPSILON = 1e-06


def carried_in(part, axis, combine, identity):
    place = lax.axis_index(axis)
    gathered = jax.tree.map(lambda a: lax.all_gather(a, axis), part)
    state = jax.tree.map(lambda a, e: jnp.zeros_like(a) + jnp.asarray(e, a.dtype), part, identity)

    def one(step, state):
        return combine(
            state, jax.tree.map(lambda a: lax.dynamic_index_in_dim(a, step, 0, False), gathered)
        )

    return lax.fori_loop(0, place, one, state)


def segment_ids(prompt_lengths, positions):
    boundary = jnp.cumsum(prompt_lengths)
    return jnp.sum((positions[:, None] >= boundary[None, :]).astype(jnp.int32), axis=1)


def combine_pairs(earlier, later):
    return (earlier[0] * later[0], later[0][:, None, None] * earlier[1] + later[1])


def local(
    query_in,
    key_in,
    value_in,
    log_decay,
    norm_gain,
    prompt_lengths,
    step_query,
    step_key,
    step_value,
    step_decay,
    row_prompt,
):
    tok_count = query_in.shape[0]
    heads_here = log_decay.shape[1]
    nblocks = tok_count // BLOCK
    first = lax.axis_index("seq") * tok_count
    positions = first + jnp.arange(tok_count, dtype=jnp.int32)
    segs = segment_ids(prompt_lengths, positions)
    seg_entry = jnp.where(first > 0, segment_ids(prompt_lengths, (first - 1)[None])[0], -1)
    shape4 = (nblocks, BLOCK, heads_here, HDIM)
    queries = query_in.reshape(shape4)
    keys_blk = key_in.reshape(shape4)
    values_blk = value_in.reshape(shape4)
    cumul = jnp.cumsum(log_decay.reshape(nblocks, BLOCK, heads_here), axis=1)
    seg_blocks = segs.reshape(nblocks, BLOCK)
    seg_front = jnp.concatenate([seg_entry[None], seg_blocks[:-1, -1]])
    causal = jnp.arange(BLOCK)[:, None] >= jnp.arange(BLOCK)[None, :]
    linked = (causal[None] & (seg_blocks[:, :, None] == seg_blocks[:, None, :]))[:, None]
    cum_heads = jnp.transpose(cumul, (0, 2, 1))
    spread = cum_heads[:, :, :, None] - cum_heads[:, :, None, :]
    factor = jnp.where(linked, jnp.exp(jnp.where(linked, spread, 0.0)), 0.0)
    scores = jnp.einsum("nthd,nshd->nhts", queries, keys_blk, preferred_element_type=jnp.float32)
    weights = (scores * factor).astype(jnp.bfloat16)
    inner = jnp.einsum("nhts,nshd->nthd", weights, values_blk, preferred_element_type=jnp.float32)
    keep = (
        jnp.exp(cumul[:, -1:, :] - cumul)
        * (seg_blocks == seg_blocks[:, -1:]).astype(jnp.float32)[:, :, None]
    )
    keyed = (keys_blk.astype(jnp.float32) * keep[..., None]).astype(jnp.bfloat16)
    updates = jnp.einsum("nshd,nshe->nhde", keyed, values_blk, preferred_element_type=jnp.float32)
    onward = (
        jnp.exp(cumul[:, -1, :]) * (seg_blocks[:, -1] == seg_front).astype(jnp.float32)[:, None]
    )
    local_states = [jnp.zeros((heads_here, HDIM, HDIM), jnp.float32)]
    growth = [jnp.ones((heads_here,), jnp.float32)]
    blk_index = 0
    local_states.append(onward[blk_index][:, None, None] * local_states[-1] + updates[blk_index])
    growth.append(onward[blk_index] * growth[-1])
    summary = (growth[-1], local_states[-1])
    identity = (
        jnp.ones((heads_here,), jnp.float32),
        jnp.zeros((heads_here, HDIM, HDIM), jnp.float32),
    )
    entry = carried_in(summary, "seq", combine_pairs, identity)
    entry_state = entry[1]
    start_states = jnp.stack([local_states[0] + growth[0][:, None, None] * entry_state])
    state_half = start_states.astype(jnp.bfloat16)
    carried = jnp.exp(cumul) * (seg_blocks == seg_front[:, None]).astype(jnp.float32)[:, :, None]
    outer = (
        jnp.einsum("nthd,nhde->nthe", queries, state_half, preferred_element_type=jnp.float32)
        * carried[..., None]
    )
    mixed = (inner + outer).reshape(tok_count, heads_here * HDIM)
    squares = lax.psum(jnp.sum(mixed * mixed, axis=1), "head")
    scale = lax.rsqrt(squares / (HEAD_COUNT * HDIM) + EPSILON)
    attn_out = (mixed * scale[:, None] * norm_gain[None, :]).astype(jnp.bfloat16)
    boundary = jnp.cumsum(prompt_lengths)

    def prompt_end(prompt):
        last_tok = boundary[prompt] - 1
        local_tok = last_tok - first
        owned = (local_tok >= 0) & (local_tok < tok_count)
        safe_tok = jnp.clip(local_tok, 0, tok_count - 1)
        blk_index = safe_tok // BLOCK
        offset = safe_tok - blk_index * BLOCK
        cum_blk = cumul[blk_index]
        reached = cum_blk[offset]
        taken = (jnp.arange(BLOCK) <= offset) & (seg_blocks[blk_index] == prompt)
        keep_end = (
            jnp.exp(jnp.where(taken[:, None], reached[None, :] - cum_blk, 0.0))
            * taken.astype(jnp.float32)[:, None]
        )
        tailed = (keys_blk[blk_index].astype(jnp.float32) * keep_end[:, :, None]).astype(
            jnp.bfloat16
        )
        part = jnp.einsum(
            "shd,she->hde", tailed, values_blk[blk_index], preferred_element_type=jnp.float32
        )
        lead = jnp.exp(reached) * (seg_front[blk_index] == prompt).astype(jnp.float32)
        total = lead[:, None, None] * start_states[blk_index] + part
        return total * owned.astype(jnp.float32)

    candidates = lax.map(prompt_end, jnp.arange(PROMPTS, dtype=jnp.int32))
    prompt_state = lax.psum(candidates, "seq")
    rows_here = row_prompt.shape[0]
    row_states = jnp.take(prompt_state, row_prompt, axis=0)
    results = []
    for section in range(step_query.shape[0]):
        query_now = step_query[section].astype(jnp.float32).reshape(rows_here, heads_here, HDIM)
        key_now = step_key[section].astype(jnp.float32).reshape(rows_here, heads_here, HDIM)
        value_now = step_value[section].astype(jnp.float32).reshape(rows_here, heads_here, HDIM)
        row_states = (
            jnp.exp(step_decay[section])[:, :, None, None] * row_states
            + key_now[:, :, :, None] * value_now[:, :, None, :]
        )
        results.append(
            jnp.einsum(
                "rhd,rhde->rhe", query_now, row_states, precision=lax.Precision.HIGHEST
            ).reshape(rows_here, heads_here * HDIM)
        )
    decoded = jnp.stack(results)
    step_squares = lax.psum(jnp.sum(decoded * decoded, axis=2), "head")
    step_scale = lax.rsqrt(step_squares / (HEAD_COUNT * HDIM) + EPSILON)
    decode_out = (decoded * step_scale[:, :, None] * norm_gain[None, None, :]).astype(jnp.bfloat16)
    return (attn_out, decode_out)


def solution(mesh):
    in_specs = (
        P("seq", "head"),
        P("seq", "head"),
        P("seq", "head"),
        P("seq", "head"),
        P("head"),
        P(),
        P(None, "seq", "head"),
        P(None, "seq", "head"),
        P(None, "seq", "head"),
        P(None, "seq", "head"),
        P("seq"),
    )
    out_specs = (P("seq", "head"), P(None, "seq", "head"))
    return jax.shard_map(local, mesh=mesh, in_specs=in_specs, out_specs=out_specs, check_vma=False)
```

profile of v0, /device:TPU:0, one launch (start us, length us, event | category | flops | bytes accessed | tf_op | source)
XLA Modules:
  0.0 465.3 jit_solution(464305001508278530)
XLA Ops:
  7.2 0.8 copy_bitcast_fusion
  8.8 0.8 reduce-window.10
  13.3 1.5 copy.146
  14.8 2.6 convolution_add_fusion.1
  17.6 1.5 copy.133
  19.1 1.4 copy.135
  20.5 22.7 %all-gather = f32[8,1,16]{2,1,0:T(1,128)S(1)} all-gather(f32[1,1,16]{2,1,0:T(1,128)S(1)} %get-tuple-element.344), channel_id=2, replica_groups=mesh['seq'=8,'head'=4] {'seq'}, dimensions={0}, use_global_device_ids=true | all-gather | bytes 576 | tf_op jit(solution)/shard_map/all_gather | solution.py:15
  43.2 101.7 %all-gather.4.cloned.1.call-done = f32[128,128,128]{2,1,0:T(8,128)} async-done(((f32[16,128,128]{2,1,0:T(8,128)}), f32[128,128,128]{2,1,0:T(8,128)}) %all-gather.4.cloned.1.call-update) | async-done | bytes 8388624 | tf_op jit(solution)/shard_map/all_gather | solution.py:15
  145.0 32.4 %while.26 = (s32[]{:T(128)}, f32[4,16,128,128]{3,2,1,0:T(8,128)}, s32[4]{0:T(128)S(1)}, s32[4]{0:T(128)S(1)}, s32[]{:T(128)}, /*index=5*/f32[1,256,16]{1,2,0:T(8...) while((s32[]{:T(128)}, f32[4,16,128,128]{3,2,1,0:T(8,128)}, ...), condition=%wide.region_10.11_spmd, body=%wide.region_9.10_spmd.sunk | while | flops 136590384 | bytes 4248923 | solution.py:128
  149.0 0.7 compare_reduce_fusion.2
  150.4 2.7 fusion.78
  157.2 0.7 compare_reduce_fusion.2
  158.6 2.6 fusion.78
  165.2 0.7 compare_reduce_fusion.2
  166.7 2.7 fusion.78
  173.3 0.7 compare_reduce_fusion.2
  174.7 2.6 fusion.78
  177.4 1.6 convert_bitcast_fusion.1
  179.7 1.7 convert_bitcast_fusion
  182.1 0.7 copy.153
  182.7 0.7 copy.154
  183.4 1.6 fusion.54
  185.0 1.6 reshape.536
  186.6 1.6 reshape.534
  188.2 1.6 copy.155
  189.8 1.6 copy.156
  191.4 1.6 reshape.538
  193.0 0.7 copy.157
  193.7 1.6 copy.158
  195.2 0.8 reshape.540
  196.8 1.4 exponential_bitcast_fusion
  198.2 4.4 fusion.36
  202.6 4.1 multiply_reduce_fusion
  206.7 1.9 copy.131
  208.7 133.8 %all-reduce.3.cloned.1.call-done = f32[4,16,128,128]{3,2,1,0:T(8,128)} async-done(((f32[4,16,128,128]{3,2,1,0:T(8,128)}), f32[4,16,128,128]{3,2,1,0:T(8,128)}) %all-reduce.3.cloned.1.call-update) | async-done | bytes 4194320 | tf_op jit(solution)/shard_map/psum | solution.py:129
  342.5 10.0 %gather_fusion = f32[16,16,128,128]{3,2,1,0:T(8,128)} fusion(f32[4,16,128,128]{3,2,1,0:T(8,128)} %all-reduce.3.cloned.1.call-done, s32[1024]{0:T(1024)S(1)} %pad_clamp_fusion), kind=kCustom, calls=%fused_computation | custom fusion | bytes 33554496 | tf_op jit(solution)/shard_map/jit(_take)/gather | solution.py:131
  352.5 17.9 %fusion.15 = f32[16,16,1,128]{3,2,1,0:T(1,128)} fusion(bf16[16,16,128,1]{2,3,1,0:T(2,128)(2,1)S(1)} %copy-done.3, f32[16,16,128]{2,1,0:T(8,128)} %bitcast.215, f32[16,16,128]{2,1,0:T(8,128)} %bitcast.212, f32[16,16]{1,0:T(8,128)S(1)} %get-tuple-element.346, f32[16,16,128,128]{3,2,1,0:T(8,128)} %gather_fusion, f32[16,16,128]{2,1,0:T(8,128)} %bitcast.208, ...), kind=kOutput, calls=%fused_computation.28 | convolution fusion | flops 79691776 | bytes 17500176 | tf_op jit(solution)/shard_map/rhd,rhde->rhe/dot_general | solution.py:142
  370.4 0.9 stack_reshape.13
  371.4 13.4 %fusion.52 = f32[16,16,1,128]{3,2,1,0:T(1,128)} fusion(bf16[16,16,128,1]{2,3,1,0:T(2,128)(2,1)S(1)} %copy-done.2, f32[16,16,128,128]{3,2,1,0:T(8,128)} %gather_fusion, f32[16,16,128]{2,1,0:T(8,128)} %bitcast.209, f32[16,16,128]{2,1,0:T(8,128)S(1)} %bitcast.207, f32[16,16]{1,0:T(8,128)} %get-tuple-element.347, pred[16]{0:T(512)(128)(4,1)} %compare_and_fusion.1), kind=kOutput, calls=%fused_computation.108 | convolution fusion | flops 67108864 | bytes 17237008 | tf_op jit(solution)/shard_map/rhd,rhde->rhe/dot_general | solution.py:142
  384.8 0.9 stack_reshape.12
  386.4 22.6 %fusion.16 = f32[16,16,1,128]{3,2,1,0:T(1,128)} fusion(bf16[16,16,128,1]{2,3,1,0:T(2,128)(2,1)} %reshape.538, f32[16,16,128]{2,1,0:T(8,128)} %bitcast.220, f32[16,16,128]{2,1,0:T(8,128)} %bitcast.218, f32[16,16]{1,0:T(8,128)} %get-tuple-element.348, f32[16,16,128]{2,1,0:T(8,128)} %bitcast.216, f32[16,16,128]{2,1,0:T(8,128)} %bitcast.213, ...), kind=kOutput, calls=%fused_computation.29 | convolution fusion | flops 92274688 | bytes 17763344 | tf_op jit(solution)/shard_map/rhd,rhde->rhe/dot_general | solution.py:142
  409.0 0.9 stack_reshape.14
  409.9 34.9 %fusion.11 = f32[16,16,1,128]{3,2,1,0:T(1,128)} fusion(bf16[16,16,128,1]{2,3,1,0:T(2,128)(2,1)S(1)} %copy-done.1, f32[16,16,128]{2,1,0:T(8,128)} %bitcast.223, f32[16,16,128]{2,1,0:T(8,128)} %bitcast.222, f32[16,16]{1,0:T(8,128)S(1)} %get-tuple-element.345, f32[16,16,128]{2,1,0:T(8,128)} %bitcast.221, f32[16,16,128]{2,1,0:T(8,128)} %bitcast.219, ...), kind=kOutput, calls=%fused_computation.21 | convolution fusion | flops 104857600 | bytes 18026512 | tf_op jit(solution)/shard_map/rhd,rhde->rhe/dot_general | solution.py:142
  444.8 0.9 stack_reshape.15
  447.8 1.2 multiply_reduce_fusion.1
  448.9 6.4 %all-reduce = (f32[256]{0:T(256)S(1)}, f32[4,16]{1,0:T(4,128)S(1)}) all-reduce(f32[256]{0:T(256)} %get-tuple-element.351, f32[4,16]{1,0:T(4,128)S(1)} %multiply_reduce_fusion.1), channel_id=1, replica_groups=mesh['seq'=8,'head'=4] {'head'}, use_global_device_ids=true, to_apply=%region_8.9 | all-reduce | flops 320 | bytes 2560 | tf_op jit(solution)/shard_map/psum | solution.py:99
  455.4 1.9 multiply_convert_fusion.4
  457.2 1.2 multiply_convert_fusion.1
  (82 shorter events, 14.1 us)
Async XLA Ops:
  7.2 191.1 %copy-start = (bf16[256,2048]{1,0:T(8,128)(2,1)S(1)}, bf16[256,2048]{1,0:T(8,128)(2,1)}, u32[]{:S(2)}) copy-start(bf16[256,2048]{1,0:T(8,128)(2,1)} %param.15) | copy-start | bytes 3145732
  7.2 137.7 %all-gather.4.cloned.1.call-start = ((), (), s32[]{:S(2)}) async-start(), calls=%async_computation.1 | async-start | bytes 9437184 | tf_op jit(solution)/shard_map/all_gather | solution.py:15
  17.5 325.0 %all-reduce.3.cloned.1.call-start = ((), (), s32[]{:S(2)}) async-start(), calls=%async_computation | async-start | bytes 8388608 | tf_op jit(solution)/shard_map/psum | solution.py:129
  145.0 51.2 %copy-start.7 = (s32[16]{0:T(128)S(1)}, s32[16]{0:T(128)}, u32[]{:S(2)}) copy-start(s32[16]{0:T(128)} %param.25) | copy-start | bytes 196
  198.1 188.2 %copy-start.6 = (f32[16,16]{1,0:T(8,128)}, f32[16,16]{1,0:T(8,128)S(1)}, u32[]{:S(2)}) copy-start(f32[16,16]{1,0:T(8,128)S(1)} %get-tuple-element.346) | copy-start | bytes 3076
  208.6 143.9 %copy-start.3 = (bf16[16,16,128,1]{2,3,1,0:T(2,128)(2,1)S(1)}, bf16[16,16,128,1]{2,3,1,0:T(2,128)(2,1)}, u32[]{:S(2)}) copy-start(bf16[16,16,128,1]{2,3,1,0:T(2,128)(2,1)} %reshape.536) | copy-start | bytes 196612
  208.7 143.8 %copy-start.4 = (f32[2,8,16,128]{3,2,1,0:T(8,128)S(1)}, f32[2,8,16,128]{3,2,1,0:T(8,128)}, u32[]{:S(2)}) copy-start(f32[2,8,16,128]{3,2,1,0:T(8,128)} %copy.151) | copy-start | bytes 393220
  352.5 18.9 %copy-start.2 = (bf16[16,16,128,1]{2,3,1,0:T(2,128)(2,1)S(1)}, bf16[16,16,128,1]{2,3,1,0:T(2,128)(2,1)}, u32[]{:S(2)}) copy-start(bf16[16,16,128,1]{2,3,1,0:T(2,128)(2,1)} %reshape.534) | copy-start | bytes 196612
  386.4 23.6 %copy-start.1 = (bf16[16,16,128,1]{2,3,1,0:T(2,128)(2,1)S(1)}, bf16[16,16,128,1]{2,3,1,0:T(2,128)(2,1)}, u32[]{:S(2)}) copy-start(bf16[16,16,128,1]{2,3,1,0:T(2,128)(2,1)} %reshape.540) | copy-start | bytes 196612
  409.9 45.4 %copy-start.5 = (f32[2048]{0:T(1024)S(1)}, f32[2048]{0:T(1024)}, u32[]{:S(2)}) copy-start(f32[2048]{0:T(1024)} %param.19) | copy-start | bytes 24580
Sparse Core Ops, SparseCore 0:
  17.6 127.2 all-gather.3
  177.5 164.8 all-reduce.2
where the time goes:
time: 467 us; the launch traced here: 465 us
  waiting for transfers between devices  235 us (50%)
  matrix products  111 us (24%)
  local copies, waits for them, and re-layouts  46.8 us (10%)
  blocking collectives  29.1 us (6%)
  between operations  15.6 us (3%)
  other arithmetic  14.4 us (3%)
  loops' own time  13.2 us (3%)
    psum x1, waiting for transfers between devices, local(): prompt_state = lax.psum(candidates, 'seq')  134 us
    all_gather x1, waiting for transfers between devices, carried_in(): gathered = jax.tree.map(lambda a: lax.all_gather(a, axis), part)  102 us
    dot_general x4, matrix products, local(): jnp.einsum('rhd,rhde->rhe', query_now, row_states, precision=lax.Precisio...  88.8 us
    all_gather x1, blocking collectives, carried_in(): gathered = jax.tree.map(lambda a: lax.all_gather(a, axis), part)  22.7 us
    another operation x1, loops' own time, local(): candidates = lax.map(prompt_end, jnp.arange(PROMPTS, dtype=jnp.int32))  13.2 us
    unnamed x28, local copies, waits for them, and re-layouts  11.6 us
    dot_general x4, matrix products, prompt_end(): jnp.einsum('shd,she->hde', tailed, values_blk[blk_index], preferred_eleme...  10.7 us
    gather x1, local copies, waits for them, and re-layouts, local(): row_states = jnp.take(prompt_state, row_prompt, axis=0)  10 us
  transfers between devices with their start and end apart: 2, of which 2 were waited for; matrix products, arithmetic and copies ran while one was open for 7% of the time, Pallas kernels for 0%

commit v1 on v0

--- a/solution.py
+++ b/solution.py
@@ -2,6 +2,7 @@
 import jax.numpy as jnp
 from jax import lax
 from jax.sharding import PartitionSpec as P
+from jax.lax import all_gather
 
 HEAD_COUNT = 64
 HDIM = 128
@@ -126,7 +127,7 @@
         return total * owned.astype(jnp.float32)
 
     candidates = lax.map(prompt_end, jnp.arange(PROMPTS, dtype=jnp.int32))
-    prompt_state = lax.psum(candidates, "seq")
+    prompt_state = jnp.sum(all_gather(candidates, "seq"), axis=0)
     rows_here = row_prompt.shape[0]
     row_states = jnp.take(prompt_state, row_prompt, axis=0)
     results = []

time: 467 us -> 959 us (2.05)
  waiting for transfers between devices: 235 us -> 717 us
  other arithmetic: 14.4 us -> 28 us
    all_gather x0 -> x1, waiting for transfers between devices: none -> 616 us  [local(): prompt_state = jnp.sum(all_gather(candidates, 'seq'), axis=0)]
    psum x1 -> x0, waiting for transfers between devices: 134 us -> none  [local(): prompt_state = lax.psum(candidates, 'seq')]
    reduce_sum x0 -> x1, other arithmetic: none -> 14.2 us  [local(): prompt_state = jnp.sum(all_gather(candidates, 'seq'), axis=0)]
  transfers between devices with their start and end apart: 2 -> 2, of which waited for: 2 -> 2; matrix products, arithmetic and copies ran while one was open for 7% -> 3% of each run, Pallas kernels for 0% -> 0%
where the time goes in v1:
time: 959 us; the launch traced here: 957 us
  waiting for transfers between devices  717 us (75%)
  matrix products  109 us (11%)
  local copies, waits for them, and re-layouts  44.2 us (5%)
  blocking collectives  29.1 us (3%)
  other arithmetic  28 us (3%)
  between operations  15.7 us (2%)
  loops' own time  13.2 us (1%)
    all_gather x1, waiting for transfers between devices, local(): prompt_state = jnp.sum(all_gather(candidates, 'seq'), axis=0)  616 us
    all_gather x1, waiting for transfers between devices, carried_in(): gathered = jax.tree.map(lambda a: lax.all_gather(a, axis), part)  102 us
    dot_general x4, matrix products, local(): jnp.einsum('rhd,rhde->rhe', query_now, row_states, precision=lax.Precisio...  87.7 us
    all_gather x1, blocking collectives, carried_in(): gathered = jax.tree.map(lambda a: lax.all_gather(a, axis), part)  22.7 us
  transfers between devices with their start and end apart: 2, of which 2 were waited for; matrix products, arithmetic and copies ran while one was open for 3% of the time, Pallas kernels for 0%

profile of v1, /device:TPU:0, one launch (start us, length us, event | category | flops | bytes accessed | tf_op | source)
XLA Modules:
  0.0 957.2 jit_solution(7456009112177897565)
XLA Ops:
  7.2 0.8 copy_bitcast_fusion
  8.8 0.8 reduce-window.10
  9.6 0.7 fusion.50
  13.4 1.5 copy.146
  14.9 2.6 convolution_add_fusion.1
  17.7 1.5 copy.133
  19.2 1.4 copy.135
  20.6 22.7 %all-gather = f32[8,1,16]{2,1,0:T(1,128)S(1)} all-gather(f32[1,1,16]{2,1,0:T(1,128)S(1)} %get-tuple-element.344), channel_id=2, replica_groups=mesh['seq'=8,'head'=4] {'seq'}, dimensions={0}, use_global_device_ids=true | all-gather | bytes 576 | tf_op jit(solution)/shard_map/all_gather | solution.py:16
  43.3 101.6 %all-gather.6.cloned.1.call-done = f32[128,128,128]{2,1,0:T(8,128)} async-done(((f32[16,128,128]{2,1,0:T(8,128)}), f32[128,128,128]{2,1,0:T(8,128)}) %all-gather.6.cloned.1.call-update) | async-done | bytes 8388624 | tf_op jit(solution)/shard_map/all_gather | solution.py:16
  145.1 32.4 %while.26 = (s32[]{:T(128)}, f32[4,16,128,128]{3,2,1,0:T(8,128)}, s32[4]{0:T(128)S(1)}, s32[4]{0:T(128)S(1)}, s32[]{:T(128)}, /*index=5*/f32[1,256,16]{1,2,0:T(8...) while((s32[]{:T(128)}, f32[4,16,128,128]{3,2,1,0:T(8,128)}, ...), condition=%wide.region_10.11_spmd, body=%wide.region_9.10_spmd.sunk | while | flops 136590384 | bytes 4248923 | solution.py:129
  149.1 0.7 compare_reduce_fusion.2
  150.5 2.7 fusion.78
  157.2 0.7 compare_reduce_fusion.2
  158.6 2.7 fusion.78
  165.3 0.7 compare_reduce_fusion.2
  166.7 2.7 fusion.78
  173.3 0.7 compare_reduce_fusion.2
  174.8 2.7 fusion.78
  177.5 1.6 convert_bitcast_fusion.1
  179.8 1.7 convert_bitcast_fusion
  181.5 0.7 copy.152
  182.1 0.7 copy.153
  182.8 0.7 copy.154
  183.5 1.6 fusion.54
  185.1 1.6 reshape.537
  186.7 1.6 reshape.535
  188.3 1.6 copy.155
  189.9 1.6 copy.156
  191.4 1.6 reshape.539
  193.0 0.7 copy.157
  193.7 1.6 copy.158
  195.3 0.7 reshape.541
  196.3 1.4 exponential_bitcast_fusion
  197.8 4.3 fusion.36
  202.1 4.0 multiply_reduce_fusion
  206.1 1.9 copy.131
  208.0 615.8 %all-gather.8.cloned.1.call-done = f32[32,16,128,128]{3,2,1,0:T(8,128)} async-done(((f32[4,16,128,128]{3,2,1,0:T(8,128)}), f32[32,16,128,128]{3,2,1,0:T(8,128)}) %all-gather.8.cloned.1.call-update) | async-done | bytes 33554448 | tf_op jit(solution)/shard_map/all_gather | solution.py:130
  823.8 14.2 %reduce_sum.48 = f32[4,16,128,128]{3,2,1,0:T(8,128)} reduce(f32[8,4,16,128,128]{4,3,2,1,0:T(8,128)} %bitcast.198, f32[]{:T(128)} %constant.128.clone.1), dimensions={0}, to_apply=%region_11.12 | reduce | flops 7340032 | bytes 37748740 | tf_op jit(solution)/shard_map/reduce_sum | solution.py:130
  838.0 10.1 %gather_fusion = f32[16,16,128,128]{3,2,1,0:T(8,128)} fusion(f32[4,16,128,128]{3,2,1,0:T(8,128)} %reduce_sum.48, s32[1024]{0:T(1024)S(1)} %pad_clamp_fusion), kind=kCustom, calls=%fused_computation | custom fusion | bytes 33554496 | tf_op jit(solution)/shard_map/jit(_take)/gather | solution.py:132
  848.2 16.7 %fusion.15 = f32[16,16,1,128]{3,2,1,0:T(1,128)S(1)} fusion(bf16[16,16,128,1]{2,3,1,0:T(2,128)(2,1)S(1)} %copy-done.5, f32[16,16,128]{2,1,0:T(8,128)S(1)} %bitcast.218, f32[16,16,128]{2,1,0:T(8,128)S(1)} %bitcast.215, f32[16,16]{1,0:T(8,128)S(1)} %get-tuple-element.346, f32[16,16,128,128]{3,2,1,0:T(8,128)} %gather_fusion, f32[16,16,128]{2,1,0:T(8,128)S(1)} %bitcast.211, ...), kind=kOutput, calls=%fused_computation.28 | convolution fusion | flops 79691776 | bytes 17500176 | tf_op jit(solution)/shard_map/rhd,rhde->rhe/dot_general | solution.py:143
  865.0 12.7 %fusion.52 = f32[16,16,1,128]{3,2,1,0:T(1,128)S(1)} fusion(bf16[16,16,128,1]{2,3,1,0:T(2,128)(2,1)S(1)} %copy-done.3, f32[16,16,128,128]{3,2,1,0:T(8,128)} %gather_fusion, f32[16,16,128]{2,1,0:T(8,128)S(1)} %bitcast.212, f32[16,16,128]{2,1,0:T(8,128)S(1)} %bitcast.208, f32[16,16]{1,0:T(8,128)S(1)} %get-tuple-element.347, ...), kind=kOutput, calls=%fused_computation.108 | convolution fusion | flops 67108864 | bytes 17237008 | tf_op jit(solution)/shard_map/rhd,rhde->rhe/dot_general | solution.py:143
  878.5 23.2 %fusion.16 = f32[16,16,1,128]{3,2,1,0:T(1,128)S(1)} fusion(bf16[16,16,128,1]{2,3,1,0:T(2,128)(2,1)S(1)} %copy-done.4, f32[16,16,128]{2,1,0:T(8,128)S(1)} %bitcast.223, f32[16,16,128]{2,1,0:T(8,128)S(1)} %bitcast.221, f32[16,16]{1,0:T(8,128)} %get-tuple-element.348, f32[16,16,128]{2,1,0:T(8,128)S(1)} %bitcast.219, f32[16,16,128]{2,1,0:T(8,128)S(1)} %bitcast.216, ...), kind=kOutput, calls=%fused_computation.29 | convolution fusion | flops 92274688 | bytes 17763344 | tf_op jit(solution)/shard_map/rhd,rhde->rhe/dot_general | solution.py:143
  901.8 35.0 %fusion.11 = f32[16,16,1,128]{3,2,1,0:T(1,128)} fusion(bf16[16,16,128,1]{2,3,1,0:T(2,128)(2,1)S(1)} %copy-done.2, f32[16,16,128]{2,1,0:T(8,128)} %bitcast.225, f32[16,16,128]{2,1,0:T(8,128)} %bitcast.224, f32[16,16]{1,0:T(8,128)S(1)} %get-tuple-element.345, f32[16,16,128]{2,1,0:T(8,128)} %bitcast.222, f32[16,16,128]{2,1,0:T(8,128)} %bitcast.220, ...), kind=kOutput, calls=%fused_computation.21 | convolution fusion | flops 104857600 | bytes 18026512 | tf_op jit(solution)/shard_map/rhd,rhde->rhe/dot_general | solution.py:143
  936.8 0.9 stack_reshape.15
  939.7 1.2 multiply_reduce_fusion.1
  940.9 6.4 all-reduce
  947.3 1.9 multiply_convert_fusion.4
  949.1 1.2 multiply_convert_fusion.1
  (101 shorter events, 12.4 us)
Async XLA Ops:
  7.2 190.6 %copy-start = (bf16[256,2048]{1,0:T(8,128)(2,1)S(1)}, bf16[256,2048]{1,0:T(8,128)(2,1)}, u32[]{:S(2)}) copy-start(bf16[256,2048]{1,0:T(8,128)(2,1)} %param.15) | copy-start | bytes 3145732
  7.2 137.8 %all-gather.6.cloned.1.call-start = ((), (), s32[]{:S(2)}) async-start(), calls=%async_computation | async-start | bytes 9437184 | tf_op jit(solution)/shard_map/all_gather | solution.py:16
  17.6 806.2 %all-gather.8.cloned.1.call-start = ((), (), s32[]{:S(2)}) async-start(), calls=%async_computation.1 | async-start | bytes 37748736 | tf_op jit(solution)/shard_map/all_gather | solution.py:130
  145.1 51.1 %copy-start.15 = (s32[16]{0:T(128)S(1)}, s32[16]{0:T(128)}, u32[]{:S(2)}) copy-start(s32[16]{0:T(128)} %param.25) | copy-start | bytes 196
  196.3 668.7 %copy-start.16 = (pred[16]{0:T(512)(128)(4,1)}, pred[16]{0:T(512)(128)(4,1)S(1)}, u32[]{:S(2)}) copy-start(pred[16]{0:T(512)(128)(4,1)S(1)} %compare_and_fusion.1) | copy-start | bytes 52
  197.6 667.3 %copy-start.14 = (f32[16,16]{1,0:T(8,128)}, f32[16,16]{1,0:T(8,128)S(1)}, u32[]{:S(2)}) copy-start(f32[16,16]{1,0:T(8,128)S(1)} %get-tuple-element.347) | copy-start | bytes 3076
  197.6 680.8 %copy-start.13 = (f32[16,16]{1,0:T(8,128)}, f32[16,16]{1,0:T(8,128)S(1)}, u32[]{:S(2)}) copy-start(f32[16,16]{1,0:T(8,128)S(1)} %get-tuple-element.346) | copy-start | bytes 3076
  838.0 10.1 %copy-start.5 = (bf16[16,16,128,1]{2,3,1,0:T(2,128)(2,1)S(1)}, bf16[16,16,128,1]{2,3,1,0:T(2,128)(2,1)}, u32[]{:S(2)}) copy-start(bf16[16,16,128,1]{2,3,1,0:T(2,128)(2,1)} %reshape.537) | copy-start | bytes 196612
  838.0 10.1 %copy-start.6 = (f32[2,8,16,128]{3,2,1,0:T(8,128)S(1)}, f32[2,8,16,128]{3,2,1,0:T(8,128)}, u32[]{:S(2)}) copy-start(f32[2,8,16,128]{3,2,1,0:T(8,128)} %copy.151) | copy-start | bytes 393220
  838.0 10.1 %copy-start.7 = (f32[2,8,16,128]{3,2,1,0:T(8,128)S(1)}, f32[2,8,16,128]{3,2,1,0:T(8,128)}, u32[]{:S(2)}) copy-start(f32[2,8,16,128]{3,2,1,0:T(8,128)} %copy.152) | copy-start | bytes 393220
  838.0 10.1 %copy-start.8 = (f32[2,8,16,128]{3,2,1,0:T(8,128)S(1)}, f32[2,8,16,128]{3,2,1,0:T(8,128)}, u32[]{:S(2)}) copy-start(f32[2,8,16,128]{3,2,1,0:T(8,128)} %copy.153) | copy-start | bytes 393220
  838.0 10.1 %copy-start.9 = (f32[2,8,16,128]{3,2,1,0:T(8,128)S(1)}, f32[2,8,16,128]{3,2,1,0:T(8,128)}, u32[]{:S(2)}) copy-start(f32[2,8,16,128]{3,2,1,0:T(8,128)} %copy.154) | copy-start | bytes 393220
  848.2 16.8 %copy-start.3 = (bf16[16,16,128,1]{2,3,1,0:T(2,128)(2,1)S(1)}, bf16[16,16,128,1]{2,3,1,0:T(2,128)(2,1)}, u32[]{:S(2)}) copy-start(bf16[16,16,128,1]{2,3,1,0:T(2,128)(2,1)} %reshape.535) | copy-start | bytes 196612
  864.9 13.6 %copy-start.4 = (bf16[16,16,128,1]{2,3,1,0:T(2,128)(2,1)S(1)}, bf16[16,16,128,1]{2,3,1,0:T(2,128)(2,1)}, u32[]{:S(2)}) copy-start(bf16[16,16,128,1]{2,3,1,0:T(2,128)(2,1)} %reshape.539) | copy-start | bytes 196612
  864.9 13.5 %copy-start.10 = (f32[2,8,16,128]{3,2,1,0:T(8,128)S(1)}, f32[2,8,16,128]{3,2,1,0:T(8,128)}, u32[]{:S(2)}) copy-start(f32[2,8,16,128]{3,2,1,0:T(8,128)} %copy.155) | copy-start | bytes 393220
  864.9 13.5 %copy-start.11 = (f32[2,8,16,128]{3,2,1,0:T(8,128)S(1)}, f32[2,8,16,128]{3,2,1,0:T(8,128)}, u32[]{:S(2)}) copy-start(f32[2,8,16,128]{3,2,1,0:T(8,128)} %copy.156) | copy-start | bytes 393220
  878.5 23.3 %copy-start.2 = (bf16[16,16,128,1]{2,3,1,0:T(2,128)(2,1)S(1)}, bf16[16,16,128,1]{2,3,1,0:T(2,128)(2,1)}, u32[]{:S(2)}) copy-start(bf16[16,16,128,1]{2,3,1,0:T(2,128)(2,1)} %reshape.541) | copy-start | bytes 196612
  901.8 45.5 %copy-start.12 = (f32[2048]{0:T(1024)S(1)}, f32[2048]{0:T(1024)}, u32[]{:S(2)}) copy-start(f32[2048]{0:T(1024)} %param.19) | copy-start | bytes 24580
  901.8 48.6 %copy-start.1 = (bf16[256,2048]{1,0:T(8,128)(2,1)S(1)}, bf16[256,2048]{1,0:T(8,128)(2,1)}, u32[]{:S(2)}) copy-start(bf16[256,2048]{1,0:T(8,128)(2,1)} %param.15) | copy-start | bytes 3145732
Sparse Core Ops, SparseCore 0:
  17.7 127.2 all-gather.5
  177.6 646.1 all-gather.7
